TPU v7x, 32 devices: a whole 2x2x4 slice. The times are simulated.
32 devices in a mesh: freq: 4 (over y, x), space: 8 (over z, core).
Axes of the slice: x: 2, y: 2, z: 4, core: 2. Of those that a mesh axis runs over, the one named last changes fastest.
Arguments:
- spectra: bfloat16 [64, 24576, 256], P('freq', 'space'), may hold values from -48 to 48, as said below
- weight: float32 [24576], P('space'), may hold values from 0.25 to 4
- partner: int32 [64], P('freq'), may hold values from 0 to 15
- counts: int32 [64], P('freq'), may hold values from 1 to 8
Outputs:
- modes: bfloat16 [64, 16, 24576], P('freq', None, 'space')
- energy: float32 [64, 8], P('freq')
- coherence: float32 [64, 2, 8, 8], P('freq')
Inputs may be any that keep to these rules, and one draw needn't show every extreme that they name: spectra are finite Fourier coefficients.
All inputs are finite; a program needn't handle non-finite values.
Results may differ from a plain program's by a relative error of at most 0.0045.
Values may be sent and summed in bfloat16 or wider, within the bound.
A program may use at most 128 MiB of HBM per device.

v0:
```python
import jax
import jax.numpy as jnp
from jax import lax
from jax.sharding import PartitionSpec as P

KMAX = 8
ITERS = 4


def from_partner(block, axis, apart):
    count = lax.axis_size(axis)
    route = []
    for low in range(count):
        high = low | 1 << apart
        if high != low and high < count:
            route += [(low, high), (high, low)]
    return lax.ppermute(block, axis, route)


def embed(gram_re, gram_im):
    top = jnp.concatenate([gram_re, -gram_im], axis=2)
    bottom = jnp.concatenate([gram_im, gram_re], axis=2)
    return jnp.concatenate([top, bottom], axis=1)


def apply_operator(operator, basis):
    return jnp.einsum("fkc,fdc->fkd", basis, operator, precision=lax.Precision.HIGHEST)


def orthonormal(vectors, half):
    done = []
    for index in range(vectors.shape[1]):
        vector = vectors[:, index, :]
        for earlier in done:
            early_re, early_im = (earlier[:, :half], earlier[:, half:])
            vec_re, vec_im = (vector[:, :half], vector[:, half:])
            proj_re = jnp.sum(early_re * vec_re + early_im * vec_im, axis=1, keepdims=True)
            proj_im = jnp.sum(early_re * vec_im - early_im * vec_re, axis=1, keepdims=True)
            new_re = vec_re - proj_re * early_re + proj_im * early_im
            new_im = vec_im - proj_re * early_im - proj_im * early_re
            vector = jnp.concatenate([new_re, new_im], axis=1)
        length = jnp.sqrt(jnp.sum(vector * vector, axis=1, keepdims=True) + 1e-06)
        done.append(vector / length)
    return jnp.stack(done, axis=1)


def solve(gram_re, gram_im):
    half = gram_re.shape[1]
    operator = embed(gram_re, gram_im)
    basis = jnp.broadcast_to(
        jnp.eye(KMAX, 2 * half, dtype=jnp.float32), (gram_re.shape[0], KMAX, 2 * half)
    )
    for sweep in range(ITERS):
        basis = orthonormal(apply_operator(operator, basis), half)
    image = apply_operator(operator, basis)
    energy = jnp.sum(basis * image, axis=2)
    return (basis, energy)


def combine(moments, half, total):
    gram_re = (moments[:, :half, :half] + moments[:, half:, half:]) / total
    gram_im = (moments[:, :half, half:] - moments[:, half:, :half]) / total
    return (gram_re, gram_im)


def coefficients(basis, energy, counts):
    half = basis.shape[2] // 2
    ranks = jnp.arange(KMAX, dtype=jnp.int32)[None, :]
    scale = jnp.where(ranks < counts[:, None], 1.0 / jnp.sqrt(energy + 1e-06), 0.0)[:, :, None]
    part_re, part_im = (basis[:, :, :half], basis[:, :, half:])
    upper = jnp.concatenate([part_re, -part_im], axis=2) * scale
    lower = jnp.concatenate([part_im, part_re], axis=2) * scale
    return jnp.concatenate([upper, lower], axis=1).astype(jnp.bfloat16)


def cross_terms(own_modes, other_modes, point_weight, total):
    phi = own_modes.astype(jnp.float32)
    psi = other_modes.astype(jnp.float32)
    wphi = phi * point_weight[None, None, :]
    highest = lax.Precision.HIGHEST

    def inner(left, right):
        return jnp.einsum("fkp,flp->fkl", left, right, precision=highest)

    real_part = inner(wphi[:, :KMAX], psi[:, :KMAX]) + inner(wphi[:, KMAX:], psi[:, KMAX:])
    imag_part = inner(wphi[:, :KMAX], psi[:, KMAX:]) - inner(wphi[:, KMAX:], psi[:, :KMAX])
    return jnp.stack([real_part, imag_part], axis=1) / total


def on_device(spectra, weight, partner, counts):
    groups = spectra.shape[0]
    half = spectra.shape[2] // 2
    total = spectra.shape[1] * lax.axis_size("space")
    weighted = (weight[None, :, None] * spectra).astype(jnp.bfloat16)
    moments = lax.dot_general(
        spectra, weighted, (((1,), (1,)), ((0,), (0,))), preferred_element_type=jnp.float32
    )
    summed = lax.psum(moments, "space")
    gram_re, gram_im = combine(summed, half, total)
    basis, energy = solve(gram_re, gram_im)
    coefficient = coefficients(basis, energy, counts)
    modes = jnp.einsum(
        "fkc,fpc->fkp", coefficient, spectra, preferred_element_type=jnp.float32
    ).astype(jnp.bfloat16)
    levels = lax.axis_size("freq").bit_length() - 1
    mirrored = modes
    for bit in range(levels):
        mirrored = from_partner(mirrored, "freq", bit)
    match = (partner[:, None] == jnp.arange(groups, dtype=jnp.int32)[None, :]).astype(jnp.bfloat16)
    chosen = jnp.einsum("fg,gkp->fkp", match, mirrored, preferred_element_type=jnp.float32).astype(
        jnp.bfloat16
    )
    local = cross_terms(modes, chosen, weight, total)
    coherence = lax.psum(local, "space")
    return (modes, energy, coherence)


def solution(mesh):
    in_specs = (P("freq", "space", None), P("space"), P("freq"), P("freq"))
    out_specs = (P("freq", None, "space"), P("freq", None), P("freq", None, None, None))
    return jax.shard_map(
        on_device, mesh=mesh, in_specs=in_specs, out_specs=out_specs, check_vma=False
    )
```

profile of v0, /device:TPU:0, one launch (start us, length us, event | category | flops | bytes accessed | tf_op | source)
XLA Modules:
  0.0 290.2 jit_solution(2149110146235932898)
XLA Ops:
  7.2 20.7 %fusion.2 = f32[16,256,256]{1,2,0:T(8,128)} fusion(bf16[16,3072,256]{2,1,0:T(8,128)(2,1)} %param.4, f32[3072]{0:T(1024)} %param.5), kind=kOutput, calls=%fused_computation.7 | convolution fusion | flops 6480199680 | bytes 29372416 | tf_op jit(solution)/shard_map/dot_general | solution.py:95
  27.9 99.3 %all-reduce.2.cloned.1.call-done = f32[16,256,256]{1,2,0:T(8,128)} async-done(((f32[16,256,256]{1,2,0:T(8,128)}), f32[16,256,256]{1,2,0:T(8,128)}) %all-reduce.2.cloned.1.call-update) | async-done | bytes 4194320 | tf_op jit(solution)/shard_map/psum | solution.py:98
  127.2 2.8 fusion.80
  130.0 1.9 fusion.42
  132.2 0.1 add_reduce_fusion.111
  132.5 0.1 multiply_reduce_fusion.23
  132.7 0.3 add_reduce_fusion.96
  133.0 0.3 add_reduce_fusion.95
  133.4 0.1 multiply_reduce_fusion.22
  133.6 0.3 add_reduce_fusion.89
  133.8 0.2 add_reduce_fusion.94
  134.4 0.3 add_reduce_fusion.88
  134.6 0.2 add_reduce_fusion.102
  135.1 0.3 add_reduce_fusion.87
  135.4 0.3 add_reduce_fusion.86
  136.0 0.2 add_reduce_fusion.85
  136.5 0.2 add_reduce_fusion.84
  137.4 2.0 fusion.40
  140.2 0.3 add_reduce_fusion.68
  140.5 0.3 add_reduce_fusion.67
  141.1 0.3 add_reduce_fusion.61
  141.4 0.2 add_reduce_fusion.66
  141.9 0.3 add_reduce_fusion.60
  142.2 0.2 add_reduce_fusion.74
  142.7 0.3 add_reduce_fusion.59
  142.9 0.3 add_reduce_fusion.58
  143.5 0.2 add_reduce_fusion.57
  144.0 0.2 add_reduce_fusion.56
  145.0 2.0 fusion.38
  147.8 0.3 add_reduce_fusion.40
  148.1 0.3 add_reduce_fusion.39
  148.6 0.3 add_reduce_fusion.33
  148.9 0.2 add_reduce_fusion.38
  149.4 0.3 add_reduce_fusion.32
  149.7 0.2 add_reduce_fusion.46
  150.2 0.3 add_reduce_fusion.31
  150.5 0.3 add_reduce_fusion.30
  151.0 0.2 add_reduce_fusion.29
  151.6 0.2 add_reduce_fusion.28
  152.5 2.2 fusion.36
  155.5 0.3 add_reduce_fusion.12
  155.8 0.3 add_reduce_fusion.11
  156.4 0.3 add_reduce_fusion.5
  156.7 0.2 add_reduce_fusion.10
  157.2 0.3 add_reduce_fusion.4
  157.5 0.2 add_reduce_fusion.18
  157.9 0.3 add_reduce_fusion.3
  158.2 0.3 add_reduce_fusion.2
  158.8 0.2 add_reduce_fusion.1
  159.3 0.2 add_reduce_fusion
  160.3 2.0 fusion.34
  162.5 12.4 %convert_multiply_fusion = (f32[16,16,3072]{2,1,0:T(8,128)S(1)}, bf16[16,16,3072]{2,1,0:T(8,128)(2,1)}) fusion(f32[3072]{0:T(1024)S(1)} %copy-done, bf16[16,3072,256]{2,1,0:T(8,128)(2,1)} %param.4, bf16[16,16,256]{2,0,1:T(8,128)(2,1)S(1)} %pad_maximum_fusion), kind=kOutput, calls=%fused_computation.6 | convolution fusion | flops 405012480 | bytes 30027776 | tf_op jit(solution)/shard_map/fkc,fpc->fkp/dot_general | solution.py:102
  175.0 1.5 collective-permute-start
  176.5 34.6 %collective-permute-done = bf16[16,16,3072]{2,1,0:T(8,128)(2,1)S(1)} collective-permute-done((bf16[16,16,3072]{2,1,0:T(8,128)(2,1)}, bf16[16,16,3072]{2,1,0:T(8,128)(2,1)S(1)}, u32[]{:S(2)}, u32[]{:S(2)}) %collective-permute-start) | collective-permute-done | bytes 1572896 | tf_op jit(solution)/shard_map/ppermute | solution.py:17
  211.1 1.5 collective-permute-start.1
  212.6 33.6 %collective-permute-done.1 = bf16[16,16,3072]{2,1,0:T(8,128)(2,1)S(1)} collective-permute-done((bf16[16,16,3072]{2,1,0:T(8,128)(2,1)S(1)}, bf16[16,16,3072]{2,1,0:T(8,128)(2,1)S(1)}, u32[]{:S(2)}, u32[]{:S(2)}) %collective-permute-start.1) | collective-permute-done | bytes 1572896 | tf_op jit(solution)/shard_map/ppermute | solution.py:17
  246.1 1.9 convolution_convert_fusion
  248.0 0.1 fusion.82
  248.1 1.8 fusion.6
  249.9 1.8 fusion.4
  251.7 1.5 fusion.15
  253.2 1.8 fusion.21
  255.0 27.5 %psum.15 = f32[16,2,8,8]{3,2,0,1:T(8,128)S(1)} all-reduce(f32[16,2,8,8]{3,2,0,1:T(8,128)S(1)} %maximum_multiply_fusion.2), channel_id=1, replica_groups=mesh['freq'=4,'space'=8] {'space'}, use_global_device_ids=true, to_apply=%region_258.259 | all-reduce | flops 2048 | bytes 16384 | tf_op jit(solution)/shard_map/psum | solution.py:114
  282.6 0.7 copy.52
  (199 shorter events, 11.7 us)
Async XLA Ops:
  7.2 120.1 %all-reduce.2.cloned.1.call-start = ((), (), s32[]{:S(2)}) async-start(), calls=%async_computation | async-start | bytes 8388608 | tf_op jit(solution)/shard_map/psum | solution.py:98
  158.5 3.9 %copy-start.2 = (s32[16]{0:T(128)S(1)}, s32[16]{0:T(128)}, u32[]{:S(2)}) copy-start(s32[16]{0:T(128)} %param.7) | copy-start | bytes 196
  160.0 2.6 copy-start
  162.4 12.6 %copy-start.1 = (f32[16,8]{0,1:T(8,128)}, f32[16,8]{0,1:T(8,128)S(1)}, u32[]{:S(2)}) copy-start(f32[16,8]{0,1:T(8,128)S(1)} %fusion.33) | copy-start | bytes 1540
  162.5 83.6 %copy-start.3 = (s32[16]{0:T(128)S(1)}, s32[16]{0:T(128)}, u32[]{:S(2)}) copy-start(s32[16]{0:T(128)} %param.6) | copy-start | bytes 196
  175.0 36.1 %collective-permute-start = (bf16[16,16,3072]{2,1,0:T(8,128)(2,1)}, bf16[16,16,3072]{2,1,0:T(8,128)(2,1)S(1)}, u32[]{:S(2)}, u32[]{:S(2)}) collective-permute-start(bf16[16,16,3072]{2,1,0:T(8,128)(2,1)} %get-tuple-element.649), channel_id=1, source_target_pairs={{0,8},{8,0},{16,24},{24,16},{1,9},{9,1},{17,25},{25,17},{2,10},{10... | collective-permute-start | bytes 4718600 | tf_op jit(solution)/shard_map/ppermute | solution.py:17
  211.1 35.0 %collective-permute-start.1 = (bf16[16,16,3072]{2,1,0:T(8,128)(2,1)S(1)}, bf16[16,16,3072]{2,1,0:T(8,128)(2,1)S(1)}, u32[]{:S(2)}, u32[]{:S(2)}) collective-permute-start(bf16[16,16,3072]{2,1,0:T(8,128)(2,1)S(1)} %collective-permute-done), channel_id=1, source_target_pairs={{0,16},{16,0},{8,24},{24,8},{1,17},{17,1},{9,25},{25,9},{2,18},{18... | collective-permute-start | bytes 4718600 | tf_op jit(solution)/shard_map/ppermute | solution.py:17
Sparse Core Ops, SparseCore 0:
  28.0 99.1 all-reduce.1
where the time goes:
time: 290 us
  waiting for transfers between devices  168 us (58%)
  matrix products  51.8 us (18%)
  blocking collectives  27.5 us (9%)
  other arithmetic  24.4 us (8%)
  between operations  14.6 us (5%)
  starting transfers between devices  2.98 us (1%)
    psum x1, waiting for transfers between devices, on_device(): summed = lax.psum(moments, 'space')  99.3 us
    ppermute x2, waiting for transfers between devices, from_partner(): return lax.ppermute(block, axis, route)  68.2 us
    psum x1, blocking collectives, on_device(): coherence = lax.psum(local, 'space')  27.5 us
    dot_general x1, matrix products, on_device(): lax.dot_general(spectra, weighted, (((1,), (1,)), ((0,), (0,))), preferre...  20.7 us
    dot_general x1, matrix products, on_device(): jnp.einsum('fkc,fpc->fkp', coefficient, spectra, preferred_element_type=j...  12.4 us
    reduce_sum x44, other arithmetic, orthonormal(): jnp.sum(early_re * vec_re + early_im * vec_im, axis=1, keepdims=True)  10.6 us
    dot_general x5, matrix products, apply_operator(): jnp.einsum('fkc,fdc->fkd', basis, operator, precision=lax.Precision.HIGHEST)  9.94 us
    dot_general x4, matrix products, inner(): return jnp.einsum('fkp,flp->fkl', left, right, precision=highest)  6.86 us
  transfers between devices with their start and end apart: 3, of which 3 were waited for; matrix products, arithmetic and copies ran while one was open for 0% of the time, Pallas kernels for 0%

commit v1 on v0

--- a/solution.py
+++ b/solution.py
@@ -95,7 +95,9 @@
     moments = lax.dot_general(
         spectra, weighted, (((1,), (1,)), ((0,), (0,))), preferred_element_type=jnp.float32
     )
-    summed = lax.psum(moments, "space")
+    summed = moments
+    for hop in (1, 2, 4):
+        summed = summed + lax.ppermute(summed, "space", [(dev, dev ^ hop) for dev in range(8)])
     gram_re, gram_im = combine(summed, half, total)
     basis, energy = solve(gram_re, gram_im)
     coefficient = coefficients(basis, energy, counts)

time: 290 us -> 465 us (1.60)
  waiting for transfers between devices: 168 us -> 345 us
  between operations: 14.6 us -> 1.2 us
  starting transfers between devices: 2.98 us -> 8.97 us
    ppermute x0 -> x3, waiting for transfers between devices: none -> 278 us  [on_device(): lax.ppermute(summed, 'space', [(dev, dev ^ hop) for dev in range(8)])]
    psum x1 -> x0, waiting for transfers between devices: 99.3 us -> none  [on_device(): summed = lax.psum(moments, 'space')]
    ppermute x0 -> x3, starting transfers between devices: none -> 6.31 us  [on_device(): lax.ppermute(summed, 'space', [(dev, dev ^ hop) for dev in range(8)])]
  transfers between devices with their start and end apart: 3 -> 5, of which waited for: 3 -> 5; matrix products, arithmetic and copies ran while one was open for 0% -> 0% of each run, Pallas kernels for 0% -> 0%
where the time goes in v1:
time: 465 us
  waiting for transfers between devices  345 us (74%)
  matrix products  51.5 us (11%)
  blocking collectives  30.1 us (6%)
  other arithmetic  26.3 us (6%)
  starting transfers between devices  8.97 us (2%)
    ppermute x3, waiting for transfers between devices, on_device(): lax.ppermute(summed, 'space', [(dev, dev ^ hop) for dev in range(8)])  278 us
    ppermute x2, waiting for transfers between devices, from_partner(): return lax.ppermute(block, axis, route)  67.5 us
    psum x1, blocking collectives, on_device(): coherence = lax.psum(local, 'space')  30.1 us
    dot_general x1, matrix products, on_device(): lax.dot_general(spectra, weighted, (((1,), (1,)), ((0,), (0,))), preferre...  20.6 us
    dot_general x1, matrix products, on_device(): jnp.einsum('fkc,fpc->fkp', coefficient, spectra, preferred_element_type=j...  12.4 us
    reduce_sum x44, other arithmetic, orthonormal(): jnp.sum(early_re * vec_re + early_im * vec_im, axis=1, keepdims=True)  10.6 us
    dot_general x5, matrix products, apply_operator(): jnp.einsum('fkc,fdc->fkd', basis, operator, precision=lax.Precision.HIGHEST)  9.73 us
  transfers between devices with their start and end apart: 5, of which 5 were waited for; matrix products, arithmetic and copies ran while one was open for 0% of the time, Pallas kernels for 0%

profile of v1, /device:TPU:0, one launch (start us, length us, event | category | flops | bytes accessed | tf_op | source)
XLA Modules:
  0.0 465.2 jit_solution(6830693556247651348)
XLA Ops:
  0.6 20.6 %fusion.2 = f32[16,256,256]{1,2,0:T(8,128)} fusion(bf16[16,3072,256]{2,1,0:T(8,128)(2,1)} %param.4, f32[3072]{0:T(1024)} %param.5), kind=kOutput, calls=%fused_computation.7 | convolution fusion | flops 6480199680 | bytes 29372416 | tf_op jit(solution)/shard_map/dot_general | solution.py:95
  21.2 0.5 collective-permute-start
  21.7 7.0 %collective-permute-done = f32[16,256,256]{1,2,0:T(8,128)S(1)} collective-permute-done((f32[16,256,256]{1,2,0:T(8,128)}, f32[16,256,256]{1,2,0:T(8,128)S(1)}, u32[]{:S(2)}, u32[]{:S(2)}) %collective-permute-start) | collective-permute-done | bytes 4194336 | tf_op jit(solution)/shard_map/ppermute | solution.py:100
  28.7 3.0 add.955
  31.8 3.0 collective-permute-start.1
  34.8 90.9 %collective-permute-done.1 = f32[16,256,256]{1,2,0:T(8,128)S(1)} collective-permute-done((f32[16,256,256]{1,2,0:T(8,128)S(1)}, f32[16,256,256]{1,2,0:T(8,128)S(1)}, u32[]{:S(2)}, u32[]{:S(2)}) %collective-permute-start.1) | collective-permute-done | bytes 4194336 | tf_op jit(solution)/shard_map/ppermute | solution.py:100
  125.6 0.6 add.956
  126.3 2.8 collective-permute-start.2
  129.1 180.1 %collective-permute-done.2 = f32[16,256,256]{1,2,0:T(8,128)S(1)} collective-permute-done((f32[16,256,256]{1,2,0:T(8,128)S(1)}, f32[16,256,256]{1,2,0:T(8,128)S(1)}, u32[]{:S(2)}, u32[]{:S(2)}) %collective-permute-start.2) | collective-permute-done | bytes 4194336 | tf_op jit(solution)/shard_map/ppermute | solution.py:100
  309.2 0.6 add.957
  309.8 0.4 fusion.80
  310.2 1.9 fusion.42
  312.9 0.3 add_reduce_fusion.96
  313.2 0.3 add_reduce_fusion.95
  313.8 0.3 add_reduce_fusion.89
  314.1 0.2 add_reduce_fusion.94
  314.6 0.3 add_reduce_fusion.88
  315.3 0.3 add_reduce_fusion.87
  315.6 0.3 add_reduce_fusion.86
  316.2 0.2 add_reduce_fusion.85
  316.7 0.2 add_reduce_fusion.84
  317.6 2.0 fusion.40
  320.5 0.3 add_reduce_fusion.68
  320.8 0.3 add_reduce_fusion.67
  321.3 0.3 add_reduce_fusion.61
  321.6 0.2 add_reduce_fusion.66
  322.1 0.3 add_reduce_fusion.60
  322.9 0.3 add_reduce_fusion.59
  323.2 0.3 add_reduce_fusion.58
  323.7 0.2 add_reduce_fusion.57
  324.2 0.2 add_reduce_fusion.56
  325.2 2.0 fusion.38
  327.5 0.2 copy.164
  328.2 0.3 add_reduce_fusion.40
  328.5 0.3 add_reduce_fusion.39
  329.1 0.3 add_reduce_fusion.33
  329.4 0.2 add_reduce_fusion.38
  329.9 0.3 add_reduce_fusion.32
  330.6 0.3 add_reduce_fusion.31
  330.9 0.3 add_reduce_fusion.30
  331.5 0.2 add_reduce_fusion.29
  332.0 0.2 add_reduce_fusion.28
  332.9 2.0 fusion.36
  335.7 0.3 add_reduce_fusion.12
  336.1 0.3 add_reduce_fusion.11
  336.6 0.3 add_reduce_fusion.5
  336.9 0.2 add_reduce_fusion.10
  337.4 0.3 add_reduce_fusion.4
  338.2 0.3 add_reduce_fusion.3
  338.4 0.3 add_reduce_fusion.2
  339.0 0.2 add_reduce_fusion.1
  340.5 2.0 fusion.34
  342.8 12.4 %convert_multiply_fusion = (f32[16,16,3072]{2,1,0:T(8,128)S(1)}, bf16[16,16,3072]{2,1,0:T(8,128)(2,1)}) fusion(f32[3072]{0:T(1024)S(1)} %copy-done, bf16[16,3072,256]{2,1,0:T(8,128)(2,1)} %param.4, bf16[16,16,256]{2,0,1:T(8,128)(2,1)S(1)} %pad_maximum_fusion), kind=kOutput, calls=%fused_computation.6 | convolution fusion | flops 405012480 | bytes 30027776 | tf_op jit(solution)/shard_map/fkc,fpc->fkp/dot_general | solution.py:104
  355.2 1.4 collective-permute-start.3
  356.6 34.3 %collective-permute-done.3 = bf16[16,16,3072]{2,1,0:T(8,128)(2,1)S(1)} collective-permute-done((bf16[16,16,3072]{2,1,0:T(8,128)(2,1)}, bf16[16,16,3072]{2,1,0:T(8,128)(2,1)S(1)}, u32[]{:S(2)}, u32[]{:S(2)}) %collective-permute-start.3) | collective-permute-done | bytes 1572896 | tf_op jit(solution)/shard_map/ppermute | solution.py:17
  390.8 1.3 collective-permute-start.4
  392.1 33.3 %collective-permute-done.4 = bf16[16,16,3072]{2,1,0:T(8,128)(2,1)S(1)} collective-permute-done((bf16[16,16,3072]{2,1,0:T(8,128)(2,1)S(1)}, bf16[16,16,3072]{2,1,0:T(8,128)(2,1)S(1)}, u32[]{:S(2)}, u32[]{:S(2)}) %collective-permute-start.4) | collective-permute-done | bytes 1572896 | tf_op jit(solution)/shard_map/ppermute | solution.py:17
  425.4 1.9 convolution_convert_fusion
  427.4 1.8 fusion.6
  429.2 1.8 fusion.4
  431.0 1.5 fusion.15
  432.5 1.8 fusion.21
  434.3 30.1 %psum.7 = f32[16,2,8,8]{3,2,0,1:T(8,128)S(1)} all-reduce(f32[16,2,8,8]{3,2,0,1:T(8,128)S(1)} %maximum_multiply_fusion.2), channel_id=1, replica_groups=mesh['freq'=4,'space'=8] {'space'}, use_global_device_ids=true, to_apply=%region_257.258 | all-reduce | flops 2048 | bytes 16384 | tf_op jit(solution)/shard_map/psum | solution.py:116
  464.4 0.7 copy.52
  (205 shorter events, 13.1 us)
Async XLA Ops:
  21.2 7.5 %collective-permute-start = (f32[16,256,256]{1,2,0:T(8,128)}, f32[16,256,256]{1,2,0:T(8,128)S(1)}, u32[]{:S(2)}, u32[]{:S(2)}) collective-permute-start(f32[16,256,256]{1,2,0:T(8,128)} %fusion.2), channel_id=1, source_target_pairs={{0,1},{1,0},{2,3},{3,2},{4,5},{5,4},{6,7},{7,6},{8,9},{9,8},{10,11... | collective-permute-start | bytes 12582920 | tf_op jit(solution)/shard_map/ppermute | solution.py:100
  31.8 93.9 %collective-permute-start.1 = (f32[16,256,256]{1,2,0:T(8,128)S(1)}, f32[16,256,256]{1,2,0:T(8,128)S(1)}, u32[]{:S(2)}, u32[]{:S(2)}) collective-permute-start(f32[16,256,256]{1,2,0:T(8,128)S(1)} %add.955), channel_id=1, source_target_pairs={{0,2},{1,3},{2,0},{3,1},{4,6},{5,7},{6,4},{7,5},{8,10},{9,11},{10,... | collective-permute-start | bytes 12582920 | tf_op jit(solution)/shard_map/ppermute | solution.py:100
  126.3 182.9 %collective-permute-start.2 = (f32[16,256,256]{1,2,0:T(8,128)S(1)}, f32[16,256,256]{1,2,0:T(8,128)S(1)}, u32[]{:S(2)}, u32[]{:S(2)}) collective-permute-start(f32[16,256,256]{1,2,0:T(8,128)S(1)} %add.956), channel_id=1, source_target_pairs={{0,4},{1,5},{2,6},{3,7},{4,0},{5,1},{6,2},{7,3},{8,12},{9,13},{10,... | collective-permute-start | bytes 12582920 | tf_op jit(solution)/shard_map/ppermute | solution.py:100
  338.7 3.9 copy-start.2
  340.2 2.6 copy-start
  342.6 12.6 %copy-start.1 = (f32[16,8]{0,1:T(8,128)}, f32[16,8]{0,1:T(8,128)S(1)}, u32[]{:S(2)}) copy-start(f32[16,8]{0,1:T(8,128)S(1)} %fusion.33) | copy-start | bytes 1540
  342.8 82.6 %copy-start.3 = (s32[16]{0:T(128)S(1)}, s32[16]{0:T(128)}, u32[]{:S(2)}) copy-start(s32[16]{0:T(128)} %param.6) | copy-start | bytes 196
  355.2 35.6 %collective-permute-start.3 = (bf16[16,16,3072]{2,1,0:T(8,128)(2,1)}, bf16[16,16,3072]{2,1,0:T(8,128)(2,1)S(1)}, u32[]{:S(2)}, u32[]{:S(2)}) collective-permute-start(bf16[16,16,3072]{2,1,0:T(8,128)(2,1)} %get-tuple-element.649), channel_id=1, source_target_pairs={{0,8},{8,0},{16,24},{24,16},{1,9},{9,1},{17,25},{25,17},{2,10},{10... | collective-permute-start | bytes 4718600 | tf_op jit(solution)/shard_map/ppermute | solution.py:17
  390.8 34.6 %collective-permute-start.4 = (bf16[16,16,3072]{2,1,0:T(8,128)(2,1)S(1)}, bf16[16,16,3072]{2,1,0:T(8,128)(2,1)S(1)}, u32[]{:S(2)}, u32[]{:S(2)}) collective-permute-start(bf16[16,16,3072]{2,1,0:T(8,128)(2,1)S(1)} %collective-permute-done.3), channel_id=1, source_target_pairs={{0,16},{16,0},{8,24},{24,8},{1,17},{17,1},{9,25},{25,9},{2,18},{18... | collective-permute-start | bytes 4718600 | tf_op jit(solution)/shard_map/ppermute | solution.py:17
